TPU v7x, 32 devices: a whole 2x2x4 slice. The times are simulated.
32 devices in a mesh: row: 4 (over y, x), col: 2 (over core), layer: 4 (over z).
Axes of the slice: x: 2, y: 2, z: 4, core: 2. Of those that a mesh axis runs over, the one named last changes fastest.
Arguments:
- matrix: float32 [4096, 4096], P('row', 'col'), may hold values from -6 to 6
- pattern: int32 [128, 128], P('row', 'col'), may hold values 0 or 1
- keep: int32 [128, 128], P('row', 'col'), may hold values 0 or 1
Outputs:
- update: float32 [4096, 4096], P(('row', 'layer'), 'col')
All inputs are finite; a program needn't handle non-finite values. No bound on the sum of `pattern` or of `keep` on one device may be relied on, other than what follows from the above.
Results may differ from a plain program's by a relative error of at most 0.00005.
Values sent between devices are 32-bit elements; how exact they have to be, the bound alone decides.
A program may use at most 128 MiB of HBM per device.

v0:
```python
import jax
import jax.numpy as jnp
from jax import lax
from jax.sharding import PartitionSpec as P

BS = 32
NB = 128


def layer_rows(values, layers, level):
    count, width = values.shape
    shaped = values.reshape(count // (layers * BS), layers, BS, width)
    picked = lax.dynamic_index_in_dim(shaped, level, 1, keepdims=False)
    return picked.reshape(count // layers, width)


def local(matrix, pattern, keep):
    rows, cols = matrix.shape
    block_rows, block_cols = pattern.shape
    layers = lax.axis_size("layer")
    level = lax.axis_index("layer")
    sparse = (
        matrix.reshape(block_rows, BS, block_cols, BS)
        * pattern.astype(jnp.float32)[:, None, :, None]
    ).reshape(rows, cols)
    left_local = lax.dynamic_index_in_dim(
        sparse.reshape(rows, block_cols // layers, layers, BS), level, 2, keepdims=False
    )
    left_local = left_local.reshape(rows, block_cols // layers * BS)
    left_full = lax.all_gather(left_local, "col", axis=1, tiled=True)
    right_full = lax.all_gather(layer_rows(sparse, layers, level), "row", axis=0, tiled=True)
    partial_value = jnp.dot(
        left_full, right_full, preferred_element_type=jnp.float32, precision=lax.Precision.HIGHEST
    )
    keep_flags = keep.astype(jnp.float32)
    keep_mine = lax.dynamic_index_in_dim(
        keep_flags.reshape(block_rows // layers, layers, block_cols), level, 1, keepdims=False
    )
    square = lax.psum(partial_value, "layer")
    mine = layer_rows(square, layers, level)
    filtered = (
        mine.reshape(block_rows // layers, BS, block_cols, BS) * keep_mine[:, None, :, None]
    ).reshape(rows // layers, cols)
    filtered_full = lax.all_gather(filtered, "row", axis=0, tiled=True)
    share = rows // layers
    summed = lax.psum_scatter(
        jnp.dot(
            left_full,
            filtered_full,
            preferred_element_type=jnp.float32,
            precision=lax.Precision.HIGHEST,
        ),
        "layer",
        scatter_dimension=0,
        tiled=True,
    )
    own_rows = lax.dynamic_slice_in_dim(sparse, level * share, share, 0)
    factor = 0.72 / (NB * BS)
    return 1.5 * own_rows - 0.5 * factor * summed


def solution(mesh):
    placed = (P("row", "col"), P("row", "col"), P("row", "col"))
    return jax.shard_map(
        local, mesh=mesh, in_specs=placed, out_specs=P(("row", "layer"), "col"), check_vma=False
    )
```

profile of v0, /device:TPU:0, one launch (start us, length us, event | category | flops | bytes accessed | tf_op | source)
XLA Modules:
  0.0 727.2 jit_solution(3081529053856967968)
XLA Ops:
  6.5 0.0 all-gather.4.cloned.1.call-start
  6.5 0.7 convert_element_type.6
  7.3 9.3 %copy.4 = f32[1024,2048]{0,1:T(8,128)} copy(f32[1024,2048]{1,0:T(8,128)} %param.3) | data formatting | bytes 16777216 | tf_op args[0]
  16.5 0.1 copy.5
  16.6 0.3 mul.63
  16.9 0.5 mul.64
  17.4 0.1 constant_dynamic-slice_fusion.3
  17.5 3.3 dynamic-slice_multiply_fusion.1
  20.8 0.0 all-gather.4.cloned.1.call-update
  20.8 0.0 all-gather.6.cloned.1.call-start
  20.9 0.3 mul.67
  21.2 0.5 mul.68
  21.7 0.1 constant_dynamic-slice_fusion.2
  21.8 3.2 dynamic-slice_multiply_fusion
  25.0 0.0 all-gather.6.cloned.1.call-update
  25.0 0.0 all-reduce.2.cloned.1.call-start
  25.1 12.3 %all-gather.4.cloned.1.call-done = f32[1024,1024]{0,1:T(8,128)} async-done(((f32[1024,512]{0,1:T(8,128)}), f32[1024,1024]{0,1:T(8,128)}) %all-gather.4.cloned.1.call-update) | async-done | bytes 4194320 | tf_op jit(solution)/shard_map/all_gather | solution.py:30
  37.4 90.5 %all-gather.6.cloned.1.call-done = f32[1024,2048]{1,0:T(8,128)} async-done(((f32[256,2048]{1,0:T(8,128)}), f32[1024,2048]{1,0:T(8,128)}) %all-gather.6.cloned.1.call-update) | async-done | bytes 8388624 | tf_op jit(solution)/shard_map/all_gather | solution.py:31
  127.9 31.0 %fusion.2 = f32[1024,2048]{1,0:T(8,128)} fusion(f32[1024,1024]{0,1:T(8,128)} %all-gather.4.cloned.1.call-done, f32[1024,2048]{1,0:T(8,128)} %all-gather.6.cloned.1.call-done), kind=kOutput, calls=%fused_computation.10 | convolution fusion | flops 25769803776 | bytes 20971520 | tf_op jit(solution)/shard_map/dot_general | solution.py:32
  158.9 0.0 copy-start
  158.9 0.0 all-reduce.2.cloned.1.call-update
  159.0 0.0 all-gather.8.cloned.1.call-start
  159.0 0.6 copy-done
  159.7 4.4 mul.72
  164.0 6.9 mul.73
  170.9 279.0 %all-reduce.2.cloned.1.call-done = f32[8,4,32,2048]{3,2,1,0:T(8,128)} async-done(((f32[8,4,32,2048]{3,2,1,0:T(8,128)}), f32[8,4,32,2048]{3,2,1,0:T(8,128)}) %all-reduce.2.cloned.1.call-update) | async-done | bytes 8388624 | tf_op jit(solution)/shard_map/psum | solution.py:39
  449.9 1.7 constant_dynamic-slice_fusion.1
  451.7 1.6 bitcast_multiply_fusion
  453.3 0.0 all-gather.8.cloned.1.call-update
  453.3 0.2 reduce-scatter.2.cloned.1.call-start
  453.5 86.4 %all-gather.8.cloned.1.call-done = f32[1024,2048]{1,0:T(8,128)} async-done(((f32[256,2048]{1,0:T(8,128)}), f32[1024,2048]{1,0:T(8,128)}) %all-gather.8.cloned.1.call-update) | async-done | bytes 8388624 | tf_op jit(solution)/shard_map/all_gather | solution.py:44
  539.9 31.0 %fusion.3 = f32[1024,2048]{1,0:T(8,128)} fusion(f32[1024,1024]{0,1:T(8,128)} %all-gather.4.cloned.1.call-done, f32[1024,2048]{1,0:T(8,128)} %all-gather.8.cloned.1.call-done), kind=kOutput, calls=%fused_computation.11 | convolution fusion | flops 25769803776 | bytes 20971520 | tf_op jit(solution)/shard_map/dot_general | solution.py:47
  571.0 0.0 reduce-scatter.2.cloned.1.call-update
  571.0 11.7 %mul.57 = f32[32,32,64,32]{3,2,1,0:T(8,128)} broadcast(f32[32,64]{1,0:T(8,128)S(1)} %convert_element_type.6), dimensions={0,2} | broadcast | bytes 8396800 | tf_op jit(solution)/shard_map/mul | solution.py:23
  582.6 25.5 %mul.58 = f32[1024,2048]{1,0:T(8,128)} reshape(f32[32,32,64,32]{3,2,1,0:T(8,128)} %mul.57) | data formatting | bytes 16777216 | tf_op jit(solution)/shard_map/mul | solution.py:23
  608.1 107.7 %reduce-scatter.2.cloned.1.call-done = f32[256,2048]{1,0:T(8,128)} async-done(((f32[1024,2048]{1,0:T(8,128)}), f32[256,2048]{1,0:T(8,128)}) %reduce-scatter.2.cloned.1.call-update) | async-done | bytes 2097168 | tf_op jit(solution)/shard_map/reduce_scatter | solution.py:46
  715.7 5.0 fusion.1
  (2 shorter events, 0.0 us)
Async XLA Ops:
  6.5 30.8 %all-gather.4.cloned.1.call-start = ((), (), s32[]{:S(2)}) async-start(), calls=%async_computation.1 | async-start | bytes 6291456 | tf_op jit(solution)/shard_map/all_gather | solution.py:30
  20.8 107.1 %all-gather.6.cloned.1.call-start = ((), (), s32[]{:S(2)}) async-start(), calls=%async_computation.2 | async-start | bytes 10485760 | tf_op jit(solution)/shard_map/all_gather | solution.py:31
  25.0 424.9 %all-reduce.2.cloned.1.call-start = ((), (), s32[]{:S(2)}) async-start(), calls=%async_computation.3 | async-start | bytes 16777216 | tf_op jit(solution)/shard_map/psum | solution.py:39
  158.9 0.7 copy-start
  159.0 381.0 %all-gather.8.cloned.1.call-start = ((), (), s32[]{:S(2)}) async-start(), calls=%async_computation.4 | async-start | bytes 10485760 | tf_op jit(solution)/shard_map/all_gather | solution.py:44
  453.3 262.4 %reduce-scatter.2.cloned.1.call-start = ((), (), s32[]{:S(2)}) async-start(), calls=%async_computation.5 | async-start | bytes 10485760 | tf_op jit(solution)/shard_map/reduce_scatter | solution.py:46
Sparse Core Ops, SparseCore 0:
  20.9 16.3 all-gather.3
  39.2 88.6 all-gather.5
  159.1 290.8 all-reduce.1
  453.4 86.4 all-gather.7
  571.1 144.6 reduce-scatter.1
where the time goes:
time: 728 us; the launch traced here: 727 us
  waiting for transfers between devices  576 us (79%)
  matrix products  62.1 us (9%)
  local copies, waits for them, and re-layouts  61.9 us (9%)
  other arithmetic  13.8 us (2%)
  between operations  13.2 us (2%)
    psum x1, waiting for transfers between devices, local(): square = lax.psum(partial_value, 'layer')  279 us
    reduce_scatter x1, waiting for transfers between devices, local(): lax.psum_scatter(jnp.dot(left_full, filtered_full, preferred_element_type...  108 us
    all_gather x1, waiting for transfers between devices, local(): lax.all_gather(layer_rows(sparse, layers, level), 'row', axis=0, tiled=True)  90.5 us
    all_gather x1, waiting for transfers between devices, local(): filtered_full = lax.all_gather(filtered, 'row', axis=0, tiled=True)  86.4 us
    mul x6, local copies, waits for them, and re-layouts, local(): matrix.reshape(block_rows, BS, block_cols, BS)  38.8 us
    dot_general x1, matrix products, local(): jnp.dot(left_full, right_full, preferred_element_type=jnp.float32, precis...  31 us
    dot_general x1, matrix products, local(): jnp.dot(left_full, filtered_full, preferred_element_type=jnp.float32, pre...  31 us
  transfers between devices with their start and end apart: 5, of which 5 were waited for; matrix products, arithmetic and copies ran while one was open for 7% of the time, Pallas kernels for 0%

commit v1 on v0

--- a/solution.py
+++ b/solution.py
@@ -36,7 +36,7 @@
     keep_mine = lax.dynamic_index_in_dim(
         keep_flags.reshape(block_rows // layers, layers, block_cols), level, 1, keepdims=False
     )
-    square = lax.psum(partial_value, "layer")
+    square = jnp.sum(lax.all_gather(partial_value, "layer"), axis=0)
     mine = layer_rows(square, layers, level)
     filtered = (
         mine.reshape(block_rows // layers, BS, block_cols, BS) * keep_mine[:, None, :, None]

time: 728 us -> 1010 us (1.39)
  waiting for transfers between devices: 576 us -> 845 us
  other arithmetic: 13.8 us -> 29.8 us
    all_gather x0 -> x1, waiting for transfers between devices: none -> 549 us  [local(): square = jnp.sum(lax.all_gather(partial_value, 'layer'), axis=0)]
    psum x1 -> x0, waiting for transfers between devices: 279 us -> none  [local(): square = lax.psum(partial_value, 'layer')]
    reduce_sum x0 -> x1, other arithmetic: none -> 15.9 us  [local(): square = jnp.sum(lax.all_gather(partial_value, 'layer'), axis=0)]
  transfers between devices with their start and end apart: 5 -> 5, of which waited for: 5 -> 5; matrix products, arithmetic and copies ran while one was open for 7% -> 5% of each run, Pallas kernels for 0% -> 0%
where the time goes in v1:
time: 1010 us
  waiting for transfers between devices  845 us (84%)
  local copies, waits for them, and re-layouts  62.3 us (6%)
  matrix products  62.1 us (6%)
  other arithmetic  29.8 us (3%)
  between operations  13.2 us (1%)
    all_gather x1, waiting for transfers between devices, local(): square = jnp.sum(lax.all_gather(partial_value, 'layer'), axis=0)  549 us
    reduce_scatter x1, waiting for transfers between devices, local(): lax.psum_scatter(jnp.dot(left_full, filtered_full, preferred_element_type...  108 us
    all_gather x1, waiting for transfers between devices, local(): lax.all_gather(layer_rows(sparse, layers, level), 'row', axis=0, tiled=True)  90.5 us
    all_gather x1, waiting for transfers between devices, local(): filtered_full = lax.all_gather(filtered, 'row', axis=0, tiled=True)  85.8 us
    mul x6, local copies, waits for them, and re-layouts, local(): matrix.reshape(block_rows, BS, block_cols, BS)  38.8 us
    dot_general x1, matrix products, local(): jnp.dot(left_full, filtered_full, preferred_element_type=jnp.float32, pre...  31 us
    dot_general x1, matrix products, local(): jnp.dot(left_full, right_full, preferred_element_type=jnp.float32, precis...  31 us
  transfers between devices with their start and end apart: 5, of which 5 were waited for; matrix products, arithmetic and copies ran while one was open for 5% of the time, Pallas kernels for 0%

profile of v1, /device:TPU:0, one launch (start us, length us, event | category | flops | bytes accessed | tf_op | source)
XLA Modules:
  0.0 1012.9 jit_solution(5552732197705775513)
XLA Ops:
  6.5 0.0 all-gather.6.cloned.1.call-start
  6.5 0.7 convert_element_type.6
  7.3 0.1 copy.7
  7.3 0.3 mul.63
  7.7 0.5 mul.64
  8.2 9.3 copy.6
  17.5 0.1 constant_dynamic-slice_fusion.3
  17.5 3.3 dynamic-slice_multiply_fusion.1
  20.8 0.0 all-gather.6.cloned.1.call-update
  20.8 0.0 all-gather.8.cloned.1.call-start
  20.9 0.3 mul.67
  21.2 0.5 mul.68
  21.7 0.1 constant_dynamic-slice_fusion.2
  21.8 3.3 dynamic-slice_multiply_fusion
  25.0 0.0 all-gather.8.cloned.1.call-update
  25.1 0.0 all-gather.12.cloned.1.call-start
  25.1 12.3 %all-gather.6.cloned.1.call-done = f32[1024,1024]{0,1:T(8,128)} async-done(((f32[1024,512]{0,1:T(8,128)}), f32[1024,1024]{0,1:T(8,128)}) %all-gather.6.cloned.1.call-update) | async-done | bytes 4194320 | tf_op jit(solution)/shard_map/all_gather | solution.py:30
  37.4 90.5 %all-gather.8.cloned.1.call-done = f32[1024,2048]{1,0:T(8,128)} async-done(((f32[256,2048]{1,0:T(8,128)}), f32[1024,2048]{1,0:T(8,128)}) %all-gather.8.cloned.1.call-update) | async-done | bytes 8388624 | tf_op jit(solution)/shard_map/all_gather | solution.py:31
  127.9 31.0 %fusion.2 = f32[1024,2048]{1,0:T(8,128)} fusion(f32[1024,1024]{0,1:T(8,128)} %all-gather.6.cloned.1.call-done, f32[1024,2048]{1,0:T(8,128)} %all-gather.8.cloned.1.call-done), kind=kOutput, calls=%fused_computation.10 | convolution fusion | flops 25769803776 | bytes 20971520 | tf_op jit(solution)/shard_map/dot_general | solution.py:32
  158.9 0.0 copy-start
  158.9 0.0 all-gather.12.cloned.1.call-update
  159.0 0.2 all-gather.10.cloned.1.call-start
  159.2 0.5 copy-done
  159.7 4.3 mul.72
  164.0 7.4 mul.73
  171.5 549.0 %all-gather.12.cloned.1.call-done = f32[4096,2048]{1,0:T(8,128)} async-done(((f32[1024,2048]{1,0:T(8,128)}), f32[4096,2048]{1,0:T(8,128)}) %all-gather.12.cloned.1.call-update) | async-done | bytes 33554448 | tf_op jit(solution)/shard_map/all_gather | solution.py:39
  720.5 15.9 %reduce_sum.9 = f32[1024,2048]{1,0:T(8,128)} reduce(f32[4,1024,2048]{2,1,0:T(8,128)} %bitcast.20, f32[]{:T(128)} %constant.29.clone.1), dimensions={0}, to_apply=%region_0.1 | reduce | flops 6291456 | bytes 41943044 | tf_op jit(solution)/shard_map/reduce_sum | solution.py:39
  736.4 1.7 constant_dynamic-slice_fusion.1
  738.2 1.6 bitcast_multiply_fusion
  739.8 0.0 all-gather.10.cloned.1.call-update
  739.8 0.0 reduce-scatter.2.cloned.1.call-start
  739.8 85.8 %all-gather.10.cloned.1.call-done = f32[1024,2048]{1,0:T(8,128)} async-done(((f32[256,2048]{1,0:T(8,128)}), f32[1024,2048]{1,0:T(8,128)}) %all-gather.10.cloned.1.call-update) | async-done | bytes 8388624 | tf_op jit(solution)/shard_map/all_gather | solution.py:44
  825.6 31.0 %fusion.3 = f32[1024,2048]{1,0:T(8,128)} fusion(f32[1024,1024]{0,1:T(8,128)} %all-gather.6.cloned.1.call-done, f32[1024,2048]{1,0:T(8,128)} %all-gather.10.cloned.1.call-done), kind=kOutput, calls=%fused_computation.11 | convolution fusion | flops 25769803776 | bytes 20971520 | tf_op jit(solution)/shard_map/dot_general | solution.py:47
  856.6 0.0 reduce-scatter.2.cloned.1.call-update
  856.7 11.7 %mul.57 = f32[32,32,64,32]{3,2,1,0:T(8,128)} broadcast(f32[32,64]{1,0:T(8,128)S(1)} %convert_element_type.6), dimensions={0,2} | broadcast | bytes 8396800 | tf_op jit(solution)/shard_map/mul | solution.py:23
  868.3 25.5 %mul.58 = f32[1024,2048]{1,0:T(8,128)} reshape(f32[32,32,64,32]{3,2,1,0:T(8,128)} %mul.57) | data formatting | bytes 16777216 | tf_op jit(solution)/shard_map/mul | solution.py:23
  893.8 107.7 %reduce-scatter.2.cloned.1.call-done = f32[256,2048]{1,0:T(8,128)} async-done(((f32[1024,2048]{1,0:T(8,128)}), f32[256,2048]{1,0:T(8,128)}) %reduce-scatter.2.cloned.1.call-update) | async-done | bytes 2097168 | tf_op jit(solution)/shard_map/reduce_scatter | solution.py:46
  1001.4 5.0 fusion.1
  (2 shorter events, 0.0 us)
Async XLA Ops:
  6.5 30.8 %all-gather.6.cloned.1.call-start = ((), (), s32[]{:S(2)}) async-start(), calls=%async_computation.1 | async-start | bytes 6291456 | tf_op jit(solution)/shard_map/all_gather | solution.py:30
  20.8 107.1 %all-gather.8.cloned.1.call-start = ((), (), s32[]{:S(2)}) async-start(), calls=%async_computation.2 | async-start | bytes 10485760 | tf_op jit(solution)/shard_map/all_gather | solution.py:31
  25.1 695.4 %all-gather.12.cloned.1.call-start = ((), (), s32[]{:S(2)}) async-start(), calls=%async_computation.5 | async-start | bytes 41943040 | tf_op jit(solution)/shard_map/all_gather | solution.py:39
  158.9 0.7 copy-start
  159.0 666.7 %all-gather.10.cloned.1.call-start = ((), (), s32[]{:S(2)}) async-start(), calls=%async_computation.3 | async-start | bytes 10485760 | tf_op jit(solution)/shard_map/all_gather | solution.py:44
  739.8 261.6 %reduce-scatter.2.cloned.1.call-start = ((), (), s32[]{:S(2)}) async-start(), calls=%async_computation.4 | async-start | bytes 10485760 | tf_op jit(solution)/shard_map/reduce_scatter | solution.py:46
Sparse Core Ops, SparseCore 0:
  20.9 16.3 all-gather.5
  39.2 88.6 all-gather.7
  159.1 561.3 all-gather.11
  739.9 85.6 all-gather.9
  856.8 144.6 reduce-scatter.1

commit v2 on v0

--- a/solution.py
+++ b/solution.py
@@ -41,7 +41,12 @@
     filtered = (
         mine.reshape(block_rows // layers, BS, block_cols, BS) * keep_mine[:, None, :, None]
     ).reshape(rows // layers, cols)
-    filtered_full = lax.all_gather(filtered, "row", axis=0, tiled=True)
+    ring = [filtered]
+    for hop in range(3):
+        ring.append(lax.ppermute(ring[-1], "row", [(dev, (dev + 1) % 4) for dev in range(4)]))
+    filtered_full = jnp.roll(
+        jnp.concatenate(ring[::-1], axis=0), (lax.axis_index("row") + 1) * ring[0].shape[0], axis=0
+    )
     share = rows // layers
     summed = lax.psum_scatter(
         jnp.dot(

time: 728 us -> 790 us (1.085)
  waiting for transfers between devices: 576 us -> 628 us
  local copies, waits for them, and re-layouts: 61.9 us -> 72.2 us
    ppermute x0 -> x3, waiting for transfers between devices: none -> 140 us  [local(): lax.ppermute(ring[-1], 'row', [(dev, (dev + 1) % 4) for dev in range(4)])]
    all_gather x1 -> x0, waiting for transfers between devices: 86.4 us -> none  [local(): filtered_full = lax.all_gather(filtered, 'row', axis=0, tiled=True)]
    unnamed x3 -> x16, local copies, waits for them, and re-layouts: 9.92 us -> 19.1 us
  transfers between devices with their start and end apart: 5 -> 7, of which waited for: 5 -> 7; matrix products, arithmetic and copies ran while one was open for 7% -> 7% of each run, Pallas kernels for 0% -> 0%
where the time goes in v2:
time: 790 us; the launch traced here: 789 us
  waiting for transfers between devices  628 us (79%)
  local copies, waits for them, and re-layouts  72.2 us (9%)
  matrix products  60.1 us (8%)
  other arithmetic  14 us (2%)
  between operations  13.3 us (2%)
    psum x1, waiting for transfers between devices, local(): square = lax.psum(partial_value, 'layer')  278 us
    ppermute x3, waiting for transfers between devices, local(): lax.ppermute(ring[-1], 'row', [(dev, (dev + 1) % 4) for dev in range(4)])  140 us
    reduce_scatter x1, waiting for transfers between devices, local(): lax.psum_scatter(jnp.dot(left_full, filtered_full, preferred_element_type...  107 us
    all_gather x1, waiting for transfers between devices, local(): lax.all_gather(layer_rows(sparse, layers, level), 'row', axis=0, tiled=True)  90.5 us
    mul x6, local copies, waits for them, and re-layouts, local(): matrix.reshape(block_rows, BS, block_cols, BS)  38.7 us
    dot_general x1, matrix products, local(): jnp.dot(left_full, right_full, preferred_element_type=jnp.float32, precis...  31.1 us
    dot_general x1, matrix products, local(): jnp.dot(left_full, filtered_full, preferred_element_type=jnp.float32, pre...  29 us
    unnamed x16, local copies, waits for them, and re-layouts  19.1 us
  transfers between devices with their start and end apart: 7, of which 7 were waited for; matrix products, arithmetic and copies ran while one was open for 7% of the time, Pallas kernels for 0%

profile of v2, /device:TPU:0, one launch (start us, length us, event | category | flops | bytes accessed | tf_op | source)
XLA Modules:
  0.0 789.4 jit_solution(12203247749989544821)
XLA Ops:
  6.5 0.0 all-gather.3.cloned.1.call-start
  6.5 0.7 convert_element_type.6
  7.3 0.1 copy.5
  7.3 0.3 mul.66
  7.7 0.5 mul.67
  8.2 9.3 %copy.4 = f32[1024,2048]{0,1:T(8,128)} copy(f32[1024,2048]{1,0:T(8,128)} %param.3) | data formatting | bytes 16777216 | tf_op args[0]
  17.5 0.1 constant_dynamic-slice_fusion.3
  17.5 3.3 dynamic-slice_multiply_fusion.1
  20.8 0.0 all-gather.3.cloned.1.call-update
  20.8 0.0 all-gather.5.cloned.1.call-start
  20.9 0.3 mul.70
  21.2 0.5 mul.71
  21.7 0.1 constant_dynamic-slice_fusion.2
  21.8 3.2 dynamic-slice_multiply_fusion
  25.0 0.0 all-gather.5.cloned.1.call-update
  25.0 0.0 all-reduce.2.cloned.1.call-start
  25.1 12.3 %all-gather.3.cloned.1.call-done = f32[1024,1024]{0,1:T(8,128)} async-done(((f32[1024,512]{0,1:T(8,128)}), f32[1024,1024]{0,1:T(8,128)}) %all-gather.3.cloned.1.call-update) | async-done | bytes 4194320 | tf_op jit(solution)/shard_map/all_gather | solution.py:30
  37.4 90.5 %all-gather.5.cloned.1.call-done = f32[1024,2048]{1,0:T(8,128)} async-done(((f32[256,2048]{1,0:T(8,128)}), f32[1024,2048]{1,0:T(8,128)}) %all-gather.5.cloned.1.call-update) | async-done | bytes 8388624 | tf_op jit(solution)/shard_map/all_gather | solution.py:31
  127.9 31.1 %fusion.5 = f32[1024,2048]{1,0:T(8,128)} fusion(f32[1024,1024]{0,1:T(8,128)} %all-gather.3.cloned.1.call-done, f32[1024,2048]{1,0:T(8,128)} %all-gather.5.cloned.1.call-done), kind=kOutput, calls=%fused_computation.21 | convolution fusion | flops 25769803776 | bytes 20971520 | tf_op jit(solution)/shard_map/dot_general | solution.py:32
  159.0 0.0 copy-start.2
  159.0 0.0 all-reduce.2.cloned.1.call-update
  159.0 0.0 reduce-scatter.2.cloned.1.call-start
  159.1 0.6 copy-done.2
  159.7 4.4 mul.75
  164.1 8.0 %mul.76 = f32[256,2048]{1,0:T(8,128)} reshape(f32[8,32,64,32]{3,2,1,0:T(8,128)} %mul.75) | data formatting | bytes 4194304 | tf_op jit(solution)/shard_map/mul | solution.py:42
  172.0 278.0 %all-reduce.2.cloned.1.call-done = f32[8,4,32,2048]{3,2,1,0:T(8,128)} async-done(((f32[8,4,32,2048]{3,2,1,0:T(8,128)}), f32[8,4,32,2048]{3,2,1,0:T(8,128)}) %all-reduce.2.cloned.1.call-update) | async-done | bytes 8388624 | tf_op jit(solution)/shard_map/psum | solution.py:39
  450.0 1.7 constant_dynamic-slice_fusion.1
  451.7 1.8 bitcast_multiply_fusion
  453.5 1.5 collective-permute-start
  455.1 46.6 %collective-permute-done = f32[256,2048]{1,0:T(8,128)S(1)} collective-permute-done((f32[256,2048]{1,0:T(8,128)S(1)}, f32[256,2048]{1,0:T(8,128)S(1)}, u32[]{:S(2)}, u32[]{:S(2)}) %collective-permute-start) | collective-permute-done | bytes 2097184 | tf_op jit(solution)/shard_map/ppermute | solution.py:46
  501.7 0.0 copy-start
  501.7 1.3 copy-done
  503.0 0.6 collective-permute-start.1
  503.6 46.8 %collective-permute-done.1 = f32[256,2048]{1,0:T(8,128)} collective-permute-done((f32[256,2048]{1,0:T(8,128)S(1)}, f32[256,2048]{1,0:T(8,128)}, u32[]{:S(2)}, u32[]{:S(2)}) %collective-permute-start.1) | collective-permute-done | bytes 2097184 | tf_op jit(solution)/shard_map/ppermute | solution.py:46
  550.4 0.0 collective-permute-start.2
  550.4 0.0 copy-start.1
  550.4 46.7 %collective-permute-done.2 = f32[256,2048]{1,0:T(8,128)} collective-permute-done((f32[256,2048]{1,0:T(8,128)}, f32[256,2048]{1,0:T(8,128)}, u32[]{:S(2)}, u32[]{:S(2)}) %collective-permute-start.2) | collective-permute-done | bytes 2097184 | tf_op jit(solution)/shard_map/ppermute | solution.py:46
  597.1 1.8 constant_dynamic-update-slice_fusion.7
  598.9 1.8 constant_dynamic-update-slice_fusion.6
  600.7 0.0 copy-done.1
  600.7 0.1 constant_dynamic-update-slice_fusion.5
  600.9 0.1 constant_dynamic-update-slice_fusion.4
  601.0 0.0 copy-start.3
  601.0 2.0 constant_dynamic-update-slice_fusion.3
  603.0 1.8 constant_dynamic-update-slice_fusion.2
  604.8 0.1 constant_dynamic-update-slice_fusion.1
  605.0 0.1 constant_dynamic-update-slice_fusion
  605.1 0.0 copy-done.3
  605.1 29.0 %fusion = f32[1024,2048]{1,0:T(8,128)} fusion(f32[1024,1024]{0,1:T(8,128)S(1)} %copy-done.3, f32[2048,2048]{1,0:T(8,128)S(1)} %constant_dynamic-update-slice_fusion, s32[]{:T(128)S(6)} %select_n.28), kind=kOutput, calls=%fused_computation | convolution fusion | flops 25769803776 | bytes 20971524 | tf_op jit(solution)/shard_map/dot_general | solution.py:52
  634.1 0.0 reduce-scatter.2.cloned.1.call-update
  634.2 11.7 %mul.60 = f32[32,32,64,32]{3,2,1,0:T(8,128)} broadcast(f32[32,64]{1,0:T(8,128)S(1)} %convert_element_type.6), dimensions={0,2} | broadcast | bytes 8396800 | tf_op jit(solution)/shard_map/mul | solution.py:23
  645.8 25.4 %mul.61 = f32[1024,2048]{1,0:T(8,128)} reshape(f32[32,32,64,32]{3,2,1,0:T(8,128)} %mul.60) | data formatting | bytes 16777216 | tf_op jit(solution)/shard_map/mul | solution.py:23
  671.2 106.7 %reduce-scatter.2.cloned.1.call-done = f32[256,2048]{1,0:T(8,128)} async-done(((f32[1024,2048]{1,0:T(8,128)}), f32[256,2048]{1,0:T(8,128)}) %reduce-scatter.2.cloned.1.call-update) | async-done | bytes 2097168 | tf_op jit(solution)/shard_map/reduce_scatter | solution.py:51
  777.9 5.0 fusion.3
  (2 shorter events, 0.0 us)
Async XLA Ops:
  6.5 30.8 %all-gather.3.cloned.1.call-start = ((), (), s32[]{:S(2)}) async-start(), calls=%async_computation.1 | async-start | bytes 6291456 | tf_op jit(solution)/shard_map/all_gather | solution.py:30
  20.8 107.1 %all-gather.5.cloned.1.call-start = ((), (), s32[]{:S(2)}) async-start(), calls=%async_computation.2 | async-start | bytes 10485760 | tf_op jit(solution)/shard_map/all_gather | solution.py:31
  25.0 425.0 %all-reduce.2.cloned.1.call-start = ((), (), s32[]{:S(2)}) async-start(), calls=%async_computation.3 | async-start | bytes 16777216 | tf_op jit(solution)/shard_map/psum | solution.py:39
  159.0 0.7 copy-start.2
  159.0 618.9 %reduce-scatter.2.cloned.1.call-start = ((), (), s32[]{:S(2)}) async-start(), calls=%async_computation.4 | async-start | bytes 10485760 | tf_op jit(solution)/shard_map/reduce_scatter | solution.py:51
  453.5 48.2 %collective-permute-start = (f32[256,2048]{1,0:T(8,128)S(1)}, f32[256,2048]{1,0:T(8,128)S(1)}, u32[]{:S(2)}, u32[]{:S(2)}) collective-permute-start(f32[256,2048]{1,0:T(8,128)S(1)} %bitcast_multiply_fusion), channel_id=1, source_target_pairs={{0,8},{8,16},{16,24},{24,0},{1,9},{9,17},{17,25},{25,1},{2,10},{10... | collective-permute-start | bytes 6291464 | tf_op jit(solution)/shard_map/ppermute | solution.py:46
  501.7 1.3 copy-start
  503.0 47.4 %collective-permute-start.1 = (f32[256,2048]{1,0:T(8,128)S(1)}, f32[256,2048]{1,0:T(8,128)}, u32[]{:S(2)}, u32[]{:S(2)}) collective-permute-start(f32[256,2048]{1,0:T(8,128)S(1)} %collective-permute-done), channel_id=1, source_target_pairs={{0,8},{8,16},{16,24},{24,0},{1,9},{9,17},{17,25},{25,1},{2,10},{10... | collective-permute-start | bytes 6291464 | tf_op jit(solution)/shard_map/ppermute | solution.py:46
  550.4 46.7 %collective-permute-start.2 = (f32[256,2048]{1,0:T(8,128)}, f32[256,2048]{1,0:T(8,128)}, u32[]{:S(2)}, u32[]{:S(2)}) collective-permute-start(f32[256,2048]{1,0:T(8,128)} %collective-permute-done.1), channel_id=1, source_target_pairs={{0,8},{8,16},{16,24},{24,0},{1,9},{9,17},{17,25},{25,1},{2,10},{10... | collective-permute-start | bytes 6291464 | tf_op jit(solution)/shard_map/ppermute | solution.py:46
  550.4 50.3 %copy-start.1 = (f32[256,2048]{1,0:T(8,128)S(1)}, f32[256,2048]{1,0:T(8,128)}, u32[]{:S(2)}) copy-start(f32[256,2048]{1,0:T(8,128)} %copy-done) | copy-start | bytes 6291460
  601.0 4.1 copy-start.3
Sparse Core Ops, SparseCore 0:
  20.9 16.3 all-gather.2
  39.2 88.6 all-gather.4
  159.1 290.8 all-reduce.1
  634.3 143.5 reduce-scatter.1
